TPU v7x, 32 devices: a whole 2x2x4 slice. The times are simulated.
32 devices in a mesh: grp: 2 (over y), mode: 8 (over z, x), node: 2 (over core).
Axes of the slice: x: 2, y: 2, z: 4, core: 2. Of those that a mesh axis runs over, the one named last changes fastest.
Arguments:
- mode_basis: float32 [4096, 4096], P('mode', 'node'), may hold values from -6 to 6
- mode_scales: float32 [4096], P('mode'), may hold values from 0.003 to 0.02
- mean_log: float32 [4096], P(('node', 'mode')), may hold values from -0.5 to 0.5
- sample_seeds: int32 [4096], P('grp'), parts along dimension 0, may hold values from 0 to 1073741823
Outputs:
- modulus: float32 [4096, 4096], P(('node', 'mode'), 'grp'), parts along dimension 1
- sample_means: float32 [4096], P('grp'), parts along dimension 0
There are 2 independent parts, one for each index of `grp`. A program takes and returns all parts, laid end to end along the dimension named above; an argument that names none is the same for every part. Nothing has to cross between parts.
All inputs are finite; a program needn't handle non-finite values.
Results may differ from a plain program's by a relative error of at most 0.00005.
Values sent between devices are 32-bit elements; how exact they have to be, the bound alone decides.
A program may use at most 64 MiB of HBM per device.

v0:
```python
import math

import jax
import jax.numpy as jnp
from jax import lax
from jax.sharding import PartitionSpec as P


def scramble(seed_words, counter_words):
    mixed_word = seed_words * -1640531527 + counter_words * 668265261
    mixed_word = mixed_word ^ mixed_word >> 15 & 131071
    mixed_word = mixed_word * -2048144789
    mixed_word = mixed_word ^ mixed_word >> 13 & 524287
    mixed_word = mixed_word * -1028477387
    mixed_word = mixed_word ^ mixed_word >> 16 & 65535
    return mixed_word


def normals(sample_seeds, mode_start, mode_count):
    mode_ids = mode_start + jnp.arange(mode_count, dtype=jnp.int32)
    seed_words = sample_seeds[None, :]
    counter_words = (2 * mode_ids)[:, None]
    first_word = scramble(seed_words, counter_words)
    second_word = scramble(seed_words, counter_words + 1)
    first_unit = ((first_word & 16777215).astype(jnp.float32) + 0.5) * (1.0 / 16777216.0)
    second_unit = ((second_word & 16777215).astype(jnp.float32) + 0.5) * (1.0 / 16777216.0)
    radius = jnp.sqrt(-2.0 * jnp.log(first_unit))
    return radius * jnp.cos(2.0 * math.pi * second_unit)


def contract_all(all_modes, sample_seeds):
    mode_total = all_modes.shape[0]
    block_modes = min(512, mode_total)
    block_count = mode_total // block_modes
    start_total = jnp.zeros((all_modes.shape[1], sample_seeds.shape[0]), jnp.float32)

    def add_block(block, total):
        first_mode = (block * block_modes).astype(jnp.int32)
        rows = lax.dynamic_slice_in_dim(all_modes, first_mode, block_modes, 0)
        coeffs = normals(sample_seeds, first_mode, block_modes)
        return total + lax.dot_general(
            rows,
            coeffs,
            (((0,), (0,)), ((), ())),
            precision=lax.Precision.HIGHEST,
            preferred_element_type=jnp.float32,
        )

    return lax.fori_loop(0, block_count, add_block, start_total)


def on_device(mode_basis, mode_scales, mean_log, sample_seeds):
    own_rows = mean_log.shape[0]
    scaled = mode_scales[:, None] * mode_basis
    gathered = lax.all_to_all(scaled, "mode", split_axis=1, concat_axis=0, tiled=True)
    summed = contract_all(gathered, sample_seeds)
    modulus = jnp.exp(mean_log[:, None] + summed)
    totals = lax.psum(jnp.sum(modulus, axis=0), ("mode", "node"))
    node_count = own_rows * lax.axis_size("mode") * lax.axis_size("node")
    return (modulus, totals / node_count)


def solution(mesh):
    return jax.shard_map(
        on_device,
        mesh=mesh,
        in_specs=(P("mode", "node"), P("mode"), P(("node", "mode")), P("grp")),
        out_specs=(P(("node", "mode"), "grp"), P("grp")),
        check_vma=False,
    )
```

profile of v0, /device:TPU:0, one launch (start us, length us, event | category | flops | bytes accessed | tf_op | source)
XLA Modules:
  0.0 334.7 jit_solution(1991284625481277206)
XLA Ops:
  0.6 2.5 broadcast_multiply_fusion.1
  3.2 2.4 copy.9
  5.5 0.0 copy-start
  5.5 7.4 %all-to-all-start = ((f32[512,8,256]{2,0,1:T(8,128)}), f32[512,8,256]{2,0,1:T(8,128)}, u32[]{:S(2)}, u32[]{:S(2)}) async-start(f32[512,8,256]{2,0,1:T(8,128)} %bitcast.8), calls=%async_computation | async-start | bytes 8388608 | tf_op jit(solution)/shard_map/all_to_all | solution.py:55
  12.9 93.3 %all-to-all-done = f32[512,8,256]{2,0,1:T(8,128)} async-done(((f32[512,8,256]{2,0,1:T(8,128)}), f32[512,8,256]{2,0,1:T(8,128)}, u32[]{:S(2)}, u32[]{:S(2)}) %all-to-all-start) | async-done | bytes 4194336 | tf_op jit(solution)/shard_map/all_to_all | solution.py:55
  106.2 0.0 copy-done
  106.2 0.0 copy-start.1
  106.2 194.2 %while.16 = (s32[]{:T(128)}, f32[256,2048]{1,0:T(8,128)S(1)}, f32[4096,256]{1,0:T(8,128)}, s32[2048]{0:T(1024)S(1)}, s32[]{:T(128)}, /*index=5*/s32[]{:T(128)}, s32[]{:T(128)}, s32[]{:T(128)}) while((s32[]{:T(128)}, f32[256,2048]{1,0:T(8,128)S(1)}, f32[4096,256]{1,0:T(8,128)}, s32[2048]{0:T(1024)S(1)}, s32[]{:T(128)}, ...), condition=%wide.region_1.0_spmd.clone, body=%wide.region_0.0_spmd.clone.sunk | while | flops 3257930240 | bytes 4751509 | solution.py:49
  106.3 24.2 %fusion.75 = f32[256,2048]{1,0:T(8,128)S(1)} fusion(f32[256,2048]{1,0:T(8,128)S(1)} %get-tuple-element.179, s32[512]{0:T(512)S(1)} %get-tuple-element.168, s32[512]{0:T(512)S(1)} %get-tuple-element.169, s32[2048]{0:T(1024)S(1)} %broadcast_multiply_fusion.4, pred[]{:T(512)S(6)} %compare.3, f32[4096,256]{1,0:T(8,128)} %get-tuple-element.188, ...), kind=kOutput, calls=%fused_computation.36.clone.1 | convolution fusion | flops 3257925632 | bytes 4730885 | tf_op jit(solution)/shard_map/while/body/eval_jaxpr/dot_general | solution.py:41
  130.5 24.2 %fusion.75 = f32[256,2048]{1,0:T(8,128)S(1)} fusion(f32[256,2048]{1,0:T(8,128)S(1)} %get-tuple-element.179, s32[512]{0:T(512)S(1)} %get-tuple-element.168, s32[512]{0:T(512)S(1)} %get-tuple-element.169, s32[2048]{0:T(1024)S(1)} %broadcast_multiply_fusion.4, pred[]{:T(512)S(6)} %compare.3, f32[4096,256]{1,0:T(8,128)} %get-tuple-element.188, ...), kind=kOutput, calls=%fused_computation.36.clone.1 | convolution fusion | flops 3257925632 | bytes 4730885 | tf_op jit(solution)/shard_map/while/body/eval_jaxpr/dot_general | solution.py:41
  154.8 24.2 %fusion.75 = f32[256,2048]{1,0:T(8,128)S(1)} fusion(f32[256,2048]{1,0:T(8,128)S(1)} %get-tuple-element.179, s32[512]{0:T(512)S(1)} %get-tuple-element.168, s32[512]{0:T(512)S(1)} %get-tuple-element.169, s32[2048]{0:T(1024)S(1)} %broadcast_multiply_fusion.4, pred[]{:T(512)S(6)} %compare.3, f32[4096,256]{1,0:T(8,128)} %get-tuple-element.188, ...), kind=kOutput, calls=%fused_computation.36.clone.1 | convolution fusion | flops 3257925632 | bytes 4730885 | tf_op jit(solution)/shard_map/while/body/eval_jaxpr/dot_general | solution.py:41
  179.1 24.2 %fusion.75 = f32[256,2048]{1,0:T(8,128)S(1)} fusion(f32[256,2048]{1,0:T(8,128)S(1)} %get-tuple-element.179, s32[512]{0:T(512)S(1)} %get-tuple-element.168, s32[512]{0:T(512)S(1)} %get-tuple-element.169, s32[2048]{0:T(1024)S(1)} %broadcast_multiply_fusion.4, pred[]{:T(512)S(6)} %compare.3, f32[4096,256]{1,0:T(8,128)} %get-tuple-element.188, ...), kind=kOutput, calls=%fused_computation.36.clone.1 | convolution fusion | flops 3257925632 | bytes 4730885 | tf_op jit(solution)/shard_map/while/body/eval_jaxpr/dot_general | solution.py:41
  203.4 24.2 %fusion.75 = f32[256,2048]{1,0:T(8,128)S(1)} fusion(f32[256,2048]{1,0:T(8,128)S(1)} %get-tuple-element.179, s32[512]{0:T(512)S(1)} %get-tuple-element.168, s32[512]{0:T(512)S(1)} %get-tuple-element.169, s32[2048]{0:T(1024)S(1)} %broadcast_multiply_fusion.4, pred[]{:T(512)S(6)} %compare.3, f32[4096,256]{1,0:T(8,128)} %get-tuple-element.188, ...), kind=kOutput, calls=%fused_computation.36.clone.1 | convolution fusion | flops 3257925632 | bytes 4730885 | tf_op jit(solution)/shard_map/while/body/eval_jaxpr/dot_general | solution.py:41
  227.6 24.2 %fusion.75 = f32[256,2048]{1,0:T(8,128)S(1)} fusion(f32[256,2048]{1,0:T(8,128)S(1)} %get-tuple-element.179, s32[512]{0:T(512)S(1)} %get-tuple-element.168, s32[512]{0:T(512)S(1)} %get-tuple-element.169, s32[2048]{0:T(1024)S(1)} %broadcast_multiply_fusion.4, pred[]{:T(512)S(6)} %compare.3, f32[4096,256]{1,0:T(8,128)} %get-tuple-element.188, ...), kind=kOutput, calls=%fused_computation.36.clone.1 | convolution fusion | flops 3257925632 | bytes 4730885 | tf_op jit(solution)/shard_map/while/body/eval_jaxpr/dot_general | solution.py:41
  251.9 24.2 %fusion.75 = f32[256,2048]{1,0:T(8,128)S(1)} fusion(f32[256,2048]{1,0:T(8,128)S(1)} %get-tuple-element.179, s32[512]{0:T(512)S(1)} %get-tuple-element.168, s32[512]{0:T(512)S(1)} %get-tuple-element.169, s32[2048]{0:T(1024)S(1)} %broadcast_multiply_fusion.4, pred[]{:T(512)S(6)} %compare.3, f32[4096,256]{1,0:T(8,128)} %get-tuple-element.188, ...), kind=kOutput, calls=%fused_computation.36.clone.1 | convolution fusion | flops 3257925632 | bytes 4730885 | tf_op jit(solution)/shard_map/while/body/eval_jaxpr/dot_general | solution.py:41
  276.2 24.2 %fusion.75 = f32[256,2048]{1,0:T(8,128)S(1)} fusion(f32[256,2048]{1,0:T(8,128)S(1)} %get-tuple-element.179, s32[512]{0:T(512)S(1)} %get-tuple-element.168, s32[512]{0:T(512)S(1)} %get-tuple-element.169, s32[2048]{0:T(1024)S(1)} %broadcast_multiply_fusion.4, pred[]{:T(512)S(6)} %compare.3, f32[4096,256]{1,0:T(8,128)} %get-tuple-element.188, ...), kind=kOutput, calls=%fused_computation.36.clone.1 | convolution fusion | flops 3257925632 | bytes 4730885 | tf_op jit(solution)/shard_map/while/body/eval_jaxpr/dot_general | solution.py:41
  300.4 0.0 copy-done.1
  300.4 1.7 fusion.69
  302.1 32.0 %psum.7 = f32[2048]{0:T(1024)S(1)} all-reduce(f32[2048]{0:T(1024)S(1)} %get-tuple-element.137), channel_id=1, replica_groups=mesh['grp'=2,'mode'=8,'node'=2] {'mode','node'}, use_global_device_ids=true, to_apply=%region_3.0 | all-reduce | flops 2048 | bytes 16384 | tf_op jit(solution)/shard_map/psum | solution.py:58
  334.1 0.6 broadcast_multiply_fusion.2
  (17 shorter events, 0.1 us)
Async XLA Ops:
  5.5 100.7 %copy-start = (s32[2048]{0:T(1024)S(1)}, s32[2048]{0:T(1024)}, u32[]{:S(2)}) copy-start(s32[2048]{0:T(1024)} %param.9) | copy-start | bytes 24580
  5.5 100.7 %all-to-all-start = ((f32[512,8,256]{2,0,1:T(8,128)}), f32[512,8,256]{2,0,1:T(8,128)}, u32[]{:S(2)}, u32[]{:S(2)}) async-start(f32[512,8,256]{2,0,1:T(8,128)} %bitcast.8), calls=%async_computation | async-start | bytes 8388608 | tf_op jit(solution)/shard_map/all_to_all | solution.py:55
  106.2 194.2 %copy-start.1 = (f32[256]{0:T(256)S(1)}, f32[256]{0:T(256)}, u32[]{:S(2)}) copy-start(f32[256]{0:T(256)} %param.8) | copy-start | bytes 3076
where the time goes:
time: 335 us
  matrix products  194 us (58%)
  waiting for transfers between devices  93.3 us (28%)
  blocking collectives  32 us (10%)
  starting transfers between devices  7.41 us (2%)
  other arithmetic  4.88 us (1%)
    dot_general x8, matrix products, add_block(): lax.dot_general(rows, coeffs, (((0,), (0,)), ((), ())), precision=lax.Pre...  194 us
    all_to_all x1, waiting for transfers between devices, on_device(): lax.all_to_all(scaled, 'mode', split_axis=1, concat_axis=0, tiled=True)  93.3 us
    psum x1, blocking collectives, on_device(): totals = lax.psum(jnp.sum(modulus, axis=0), ('mode', 'node'))  32 us
    all_to_all x1, starting transfers between devices, on_device(): lax.all_to_all(scaled, 'mode', split_axis=1, concat_axis=0, tiled=True)  7.41 us
  transfers between devices with their start and end apart: 1, of which 1 were waited for; matrix products, arithmetic and copies ran while one was open for 0% of the time, Pallas kernels for 0%

commit v1 on v0

v1 whole, which is shorter than its diff:
```python
import functools
import math

import jax
import jax.numpy as jnp
import numpy as np
from jax import lax
from jax.experimental import pallas as pl
from jax.experimental.pallas import tpu as pltpu
from jax.sharding import PartitionSpec as P

MESH = pl.DeviceIdType.MESH


def sine_series():
    points = 0.25 * np.cos((np.arange(200) + 0.5) * np.pi / 400)
    powers = points[:, None] ** np.arange(0, 11, 2)[None, :]
    values = np.sin(2 * np.pi * points) / points
    return [float(c) for c in np.linalg.lstsq(powers, values, rcond=None)[0]]


SINE = sine_series()


def scramble(word):
    word = word ^ lax.shift_right_logical(word, jnp.int32(15))
    word = word * jnp.int32(-2048144789)
    word = word ^ lax.shift_right_logical(word, jnp.int32(13))
    word = word * jnp.int32(-1028477387)
    return word ^ lax.shift_right_logical(word, jnp.int32(16))


def normals(seed_terms, counter_terms):
    start_word = seed_terms + counter_terms
    first_word = scramble(start_word) & jnp.int32(16777215)
    second_word = scramble(start_word + jnp.int32(668265261)) & jnp.int32(16777215)
    first_unit = (first_word.astype(jnp.float32) + 0.5) * (1.0 / 16777216.0)
    square = -2.0 * jnp.log(first_unit)
    radius = square * lax.rsqrt(jnp.maximum(square, 1e-30))
    folded = jnp.abs(second_word.astype(jnp.float32) - 8388607.5) - 4194304.0
    turn = folded * (1.0 / 16777216.0)
    turn2 = turn * turn
    series = jnp.full_like(turn, SINE[-1])
    for coefficient in SINE[-2::-1]:
        series = series * turn2 + coefficient
    return (radius * turn) * series


def split(values):
    high = values.astype(jnp.bfloat16)
    return high, (values - high.astype(jnp.float32)).astype(jnp.bfloat16)


def kernel(n, basis, scales, mean, seeds, modulus, means, gathered, scale_all, mean_all, coef_hi, coef_lo, lhs_hi, lhs_lo,
           total, staged, parts, halves, net_send, net_recv, row_send, row_recv, core_send, core_recv,
           scale_send, scale_recv, part_send, part_recv, mean_sems, own_sem, out_sems, half_sems):
    g, me, c = lax.axis_index("grp"), lax.axis_index("mode"), lax.axis_index("node")
    _, _, _, half, wide = gathered.shape
    rows = 2 * half
    samples = coef_hi.shape[-1]
    across, sibling = (1 - g, me, c), (g, me, 1 - c)

    def to(step):
        return lax.rem(me + step, n)

    def source(step):
        return lax.rem(me + n - step, n)

    barrier = pltpu.get_barrier_semaphore()

    @pl.loop(1, n)
    def _(step):
        pl.semaphore_signal(barrier, inc=1, device_id=(g, to(step), c), device_id_type=MESH)

    pl.semaphore_signal(barrier, inc=1, device_id=across, device_id_type=MESH)
    pl.semaphore_signal(barrier, inc=1, device_id=sibling, device_id_type=MESH)

    own_scale = scale_all.at[me]
    own_mean = mean_all.at[c]
    own_scale[...] = scales[...]
    own_mean[...] = mean[...]
    own_columns = pl.ds(pl.multiple_of(me * wide, 128), wide)
    own = [
        pltpu.make_async_copy(basis.at[pl.ds(h * half, half), own_columns], gathered.at[c, me, h], own_sem.at[h])
        for h in range(2)
    ]
    for copy in own:
        copy.start()
    pl.semaphore_wait(barrier, n + 1)

    def net(step, owner):
        peer = to(step)
        return pltpu.make_async_remote_copy(
            src_ref=basis.at[pl.ds(pl.multiple_of(g * half, 8), half), pl.ds(pl.multiple_of(peer * wide, 128), wide)],
            dst_ref=gathered.at[c, owner, g],
            send_sem=net_send.at[step], recv_sem=net_recv.at[step], device_id=(g, peer, c), device_id_type=MESH)

    def scale_copy(step, owner):
        return pltpu.make_async_remote_copy(
            src_ref=scales, dst_ref=scale_all.at[owner],
            send_sem=scale_send.at[step], recv_sem=scale_recv.at[step], device_id=(g, to(step), c), device_id_type=MESH)

    def row_copy(step, owner, h):
        block = gathered.at[c, owner, h]
        return pltpu.make_async_remote_copy(
            src_ref=block, dst_ref=block,
            send_sem=row_send.at[step], recv_sem=row_recv.at[step], device_id=across, device_id_type=MESH)

    def core_copy(step, owner, h, side, which):
        block = gathered.at[side, owner, h]
        return pltpu.make_async_remote_copy(
            src_ref=block, dst_ref=block,
            send_sem=core_send.at[which, step], recv_sem=core_recv.at[which, step],
            device_id=sibling, device_id_type=MESH)

    def part_copy(step, owner):
        return pltpu.make_async_remote_copy(
            src_ref=parts.at[me], dst_ref=parts.at[owner],
            send_sem=part_send.at[step], recv_sem=part_recv.at[step], device_id=(g, to(step), c), device_id_type=MESH)

    mean_copy = lambda side: pltpu.make_async_remote_copy(
        src_ref=mean, dst_ref=mean_all.at[side], send_sem=mean_sems.at[0], recv_sem=mean_sems.at[1],
        device_id=sibling, device_id_type=MESH)

    @pl.loop(1, n)
    def _(step):
        net(step, me).start()

    @pl.loop(1, n)
    def _(step):
        scale_copy(step, me).start()

    mean_copy(c).start()
    for copy in own:
        copy.wait()
    core_copy(0, me, g, c, 0).start()
    core_copy(0, me, 1 - g, c, 1).start()

    seed_terms = seeds[:, pl.ds(pl.multiple_of(c * samples, 128), samples)] * jnp.int32(-1640531527)
    lanes = min(512, samples)

    def draw(owner):
        @pl.loop(0, rows // 16)
        def _(tile):
            first = owner * rows + tile * 16
            ids = lax.broadcasted_iota(jnp.int32, (16, lanes), 0) + first
            counters = ids * jnp.int32(2 * 668265261 - 2**32 if 2 * 668265261 >= 2**31 else 2 * 668265261)
            for start in range(0, samples, lanes):
                high, low = split(normals(seed_terms[:, start:start + lanes], counters))
                here = pl.ds(pl.multiple_of(tile * 16, 16), 16)
                coef_hi[owner, here, start:start + lanes] = high
                coef_lo[owner, here, start:start + lanes] = low

    def multiply(step, owner, first):
        core_copy(step, owner, g, 1 - c, 0).wait_recv()
        core_copy(step, owner, 1 - g, 1 - c, 1).wait_recv()
        scale_row = scale_all[owner]
        for side in range(2):
            block = gathered[side, owner].reshape(rows, wide)
            high, low = split(block.T * scale_row)
            lhs_hi[side * wide:(side + 1) * wide, :] = high
            lhs_lo[side * wide:(side + 1) * wide, :] = low
        columns = min(256, samples)

        @pl.loop(0, samples // columns)
        def _(tile):
            here = pl.ds(pl.multiple_of(tile * columns, 128), columns)
            right_hi, right_lo = coef_hi[owner, :, here], coef_lo[owner, :, here]
            dot = functools.partial(jnp.dot, preferred_element_type=jnp.float32)
            product = dot(lhs_hi[...], right_hi) + dot(lhs_lo[...], right_hi) + dot(lhs_hi[...], right_lo)
            if first:
                total[:, here] = product
            else:
                total[:, here] += product

    draw(me)

    def arrive(step):
        owner = source(step)
        net(step, owner).wait_recv()
        row_copy(step, owner, g).start()
        core_copy(step, owner, g, c, 0).start()
        draw(owner)
        row_copy(step, owner, 1 - g).wait_recv()
        core_copy(step, owner, 1 - g, c, 1).start()

    arrive(1)
    multiply(0, me, True)

    @pl.loop(2, n)
    def _(step):
        arrive(step)
        scale_copy(step - 1, source(step - 1)).wait_recv()
        multiply(step - 1, source(step - 1), False)

    scale_copy(n - 1, source(n - 1)).wait_recv()
    multiply(n - 1, source(n - 1), False)
    mean_copy(1 - c).wait_recv()

    sums = jnp.zeros((1, samples), jnp.float32)
    for side in range(2):
        shift = jnp.broadcast_to(mean_all[side], (8, wide)).T[:, :1]
        values = jnp.exp(total[side * wide:(side + 1) * wide, :] + shift)
        staged[side] = values
        sums = sums + jnp.sum(values, axis=0, keepdims=True)
    parts[me] = sums
    out_columns = modulus.at[:, pl.ds(pl.multiple_of(c * samples, 128), samples)]
    other_columns = modulus.at[:, pl.ds(pl.multiple_of((1 - c) * samples, 128), samples)]
    local_out = pltpu.make_async_copy(staged.at[c], out_columns, out_sems.at[0])
    send_out = lambda landing: pltpu.make_async_remote_copy(
        src_ref=staged.at[1 - c], dst_ref=landing, send_sem=out_sems.at[1], recv_sem=out_sems.at[2],
        device_id=sibling, device_id_type=MESH)

    @pl.loop(1, n)
    def _(step):
        part_copy(step, me).start()

    send_out(out_columns).start()
    local_out.start()

    @pl.loop(1, n)
    def _(step):
        part_copy(step, source(step)).wait_recv()

    summed = jnp.zeros((1, samples), jnp.float32)
    for m in range(n):
        summed = summed + parts[m]
    halves[c] = summed / (n * 2 * wide)
    half_copy = lambda side: pltpu.make_async_remote_copy(
        src_ref=halves.at[c], dst_ref=halves.at[side], send_sem=half_sems.at[0], recv_sem=half_sems.at[1],
        device_id=sibling, device_id_type=MESH)
    half_copy(c).start()

    mean_copy(c).wait_send()
    core_copy(0, me, g, c, 0).wait_send()
    core_copy(0, me, 1 - g, c, 1).wait_send()

    @pl.loop(1, n)
    def _(step):
        owner = source(step)
        net(step, me).wait_send()
        scale_copy(step, me).wait_send()
        part_copy(step, me).wait_send()
        row_copy(step, owner, g).wait_send()
        core_copy(step, owner, g, c, 0).wait_send()
        core_copy(step, owner, 1 - g, c, 1).wait_send()

    half_copy(1 - c).wait_recv()
    half_copy(c).wait_send()
    means[:, 0:samples] = halves[0]
    means[:, samples:2 * samples] = halves[1]
    local_out.wait()
    send_out(other_columns).wait_recv()
    send_out(out_columns).wait_send()


def on_device(mode_basis, mode_scales, mean_log, sample_seeds):
    n = lax.axis_size("mode")
    rows, wide, all_samples = mode_scales.shape[0], mean_log.shape[0], sample_seeds.shape[0]
    half, samples = rows // 2, all_samples // 2
    vmem = pl.BlockSpec(memory_space=pltpu.VMEM)
    anywhere = pl.BlockSpec(memory_space=pl.ANY)
    dma = pltpu.SemaphoreType.DMA
    modulus, means = pl.pallas_call(
        functools.partial(kernel, n),
        out_shape=(
            jax.ShapeDtypeStruct((wide, all_samples), jnp.float32),
            jax.ShapeDtypeStruct((1, all_samples), jnp.float32),
        ),
        in_specs=[anywhere, vmem, vmem, vmem],
        out_specs=(anywhere, vmem),
        scratch_shapes=[
            pltpu.VMEM((2, n, 2, half, wide), jnp.float32),
            pltpu.VMEM((n, 1, rows), jnp.float32),
            pltpu.VMEM((2, 1, wide), jnp.float32),
            pltpu.VMEM((n, rows, samples), jnp.bfloat16),
            pltpu.VMEM((n, rows, samples), jnp.bfloat16),
            pltpu.VMEM((2 * wide, rows), jnp.bfloat16),
            pltpu.VMEM((2 * wide, rows), jnp.bfloat16),
            pltpu.VMEM((2 * wide, samples), jnp.float32),
            pltpu.VMEM((2, wide, samples), jnp.float32),
            pltpu.VMEM((n, 1, samples), jnp.float32),
            pltpu.VMEM((2, 1, samples), jnp.float32),
            dma((n,)), dma((n,)), dma((n,)), dma((n,)), dma((2, n)), dma((2, n)),
            dma((n,)), dma((n,)), dma((n,)), dma((n,)), dma((2,)), dma((2,)), dma((3,)), dma((2,)),
        ],
        compiler_params=pltpu.CompilerParams(
            collective_id=0, has_side_effects=True, vmem_limit_bytes=60 * 1024 * 1024
        ),
    )(mode_basis, mode_scales[None, :], mean_log[None, :], sample_seeds[None, :])
    return modulus, means[0]


def solution(mesh):
    return jax.shard_map(
        on_device,
        mesh=mesh,
        in_specs=(P("mode", "node"), P("mode"), P(("node", "mode")), P("grp")),
        out_specs=(P(("node", "mode"), "grp"), P("grp")),
        check_vma=False,
    )
```

time: 335 us -> 111 us (0.33)
  matrix products: 194 us -> 0 us
  Pallas kernels: 0 us -> 107 us
  waiting for transfers between devices: 93.3 us -> 0 us
  blocking collectives: 32 us -> 0 us
  starting transfers between devices: 7.41 us -> 0 us
  other arithmetic: 4.88 us -> 0 us
    dot_general x8 -> x0, matrix products: 194 us -> none  [add_block(): lax.dot_general(rows, coeffs, (((0,), (0,)), ((), ())), precision=lax.Pre...]
    pallas_call x0 -> x1, Pallas kernels: none -> 107 us  [on_device(): pl.pallas_call(functools.partial(kernel, n), out_shape=(jax.ShapeDtypeStr...]
    all_to_all x1 -> x0, waiting for transfers between devices: 93.3 us -> none  [on_device(): lax.all_to_all(scaled, 'mode', split_axis=1, concat_axis=0, tiled=True)]
    psum x1 -> x0, blocking collectives: 32 us -> none  [on_device(): totals = lax.psum(jnp.sum(modulus, axis=0), ('mode', 'node'))]
    all_to_all x1 -> x0, starting transfers between devices: 7.41 us -> none  [on_device(): lax.all_to_all(scaled, 'mode', split_axis=1, concat_axis=0, tiled=True)]
    unnamed x4, local copies, waits for them, and re-layouts: 0.01 us -> 3.74 us
  transfers between devices with their start and end apart: 1 -> 0, of which waited for: 1 -> 0; matrix products, arithmetic and copies ran while one was open for 0% -> 0% of each run, Pallas kernels for 0% -> 0%
where the time goes in v1:
time: 111 us
  Pallas kernels  107 us (96%)
  local copies, waits for them, and re-layouts  3.74 us (3%)
    pallas_call x1, Pallas kernels, on_device(): pl.pallas_call(functools.partial(kernel, n), out_shape=(jax.ShapeDtypeStr...  107 us
    unnamed x4, local copies, waits for them, and re-layouts  3.74 us

profile of v1, /device:TPU:0, one launch (start us, length us, event | category | flops | bytes accessed | tf_op | source)
XLA Modules:
  0.0 110.9 jit_solution(12818201403268818274)
XLA Ops:
  0.6 106.5 %shard_map.59 = (f32[256,2048]{1,0:T(8,128)}, f32[1,2048]{1,0:T(1,128)}) custom-call(f32[512,2048]{1,0:T(8,128)} %basis.1, f32[1,512]{1,0:T(1,128)} %bitcast.6, f32[1,256]{1,0:T(1,128)} %bitcast.7, s32[1,2048]{1,0:T(1,128)} %bitcast.4), custom_call_target="tpu_custom_call" | custom-call | tf_op jit(solution)/shard_map/pallas_call | solution.py:264
  107.2 0.0 copy-start
  107.2 3.1 %copy.8 = f32[256,2048]{1,0:T(8,128)} copy(f32[256,2048]{1,0:T(8,128)} %get-tuple-element.8) | data formatting | bytes 4194304
  110.3 0.0 copy-done
  110.3 0.6 copy.9
Async XLA Ops:
  107.2 3.2 %copy-start = (f32[1,2048]{1,0:T(1,128)S(1)}, f32[1,2048]{1,0:T(1,128)}, u32[]{:S(2)}) copy-start(f32[1,2048]{1,0:T(1,128)} %get-tuple-element.5) | copy-start | bytes 24580

commit v2 on v1

--- a/solution.py
+++ b/solution.py
@@ -51,20 +51,27 @@
     return high, (values - high.astype(jnp.float32)).astype(jnp.bfloat16)
 
 
-def kernel(n, basis, scales, mean, seeds, modulus, means, gathered, scale_all, mean_all, coef_hi, coef_lo, lhs_hi, lhs_lo,
+def kernel(n, basis, scales, mean, seeds, modulus, means, gathered, scale_all, mean_all, coefs, lhs,
            total, staged, parts, halves, net_send, net_recv, row_send, row_recv, core_send, core_recv,
            scale_send, scale_recv, part_send, part_recv, mean_sems, own_sem, out_sems, half_sems):
     g, me, c = lax.axis_index("grp"), lax.axis_index("mode"), lax.axis_index("node")
-    _, _, _, half, wide = gathered.shape
-    rows = 2 * half
-    samples = coef_hi.shape[-1]
+    _, _, pieces, piece, wide = gathered.shape
+    rows = pieces * piece
+    mine, theirs = [[side * 2 + p for p in range(2)] for side in (g, 1 - g)]
+    samples = coefs.shape[-1]
     across, sibling = (1 - g, me, c), (g, me, 1 - c)
 
     def to(step):
-        return lax.rem(me + step, n)
-
-    def source(step):
-        return lax.rem(me + n - step, n)
+        flipped, bit = 0, 1
+        while bit < n:
+            flipped = flipped + lax.rem(me // bit + step // bit, 2) * bit
+            bit *= 2
+        return flipped
+
+    near, quarter = n // 2, n // 4
+
+    def far(q):
+        return near + lax.rem(q, 2) * quarter + q // 2
 
     barrier = pltpu.get_barrier_semaphore()
 
@@ -81,36 +88,36 @@
     own_mean[...] = mean[...]
     own_columns = pl.ds(pl.multiple_of(me * wide, 128), wide)
     own = [
-        pltpu.make_async_copy(basis.at[pl.ds(h * half, half), own_columns], gathered.at[c, me, h], own_sem.at[h])
-        for h in range(2)
+        pltpu.make_async_copy(basis.at[pl.ds(k * piece, piece), own_columns], gathered.at[c, me, k], own_sem.at[k])
+        for k in range(pieces)
     ]
     for copy in own:
         copy.start()
     pl.semaphore_wait(barrier, n + 1)
 
-    def net(step, owner):
+    def net(step, owner, k):
         peer = to(step)
         return pltpu.make_async_remote_copy(
-            src_ref=basis.at[pl.ds(pl.multiple_of(g * half, 8), half), pl.ds(pl.multiple_of(peer * wide, 128), wide)],
-            dst_ref=gathered.at[c, owner, g],
-            send_sem=net_send.at[step], recv_sem=net_recv.at[step], device_id=(g, peer, c), device_id_type=MESH)
+            src_ref=basis.at[pl.ds(pl.multiple_of(k * piece, 8), piece), pl.ds(pl.multiple_of(peer * wide, 128), wide)],
+            dst_ref=gathered.at[c, owner, k],
+            send_sem=net_send.at[k, step], recv_sem=net_recv.at[k, step], device_id=(g, peer, c), device_id_type=MESH)
 
     def scale_copy(step, owner):
         return pltpu.make_async_remote_copy(
             src_ref=scales, dst_ref=scale_all.at[owner],
             send_sem=scale_send.at[step], recv_sem=scale_recv.at[step], device_id=(g, to(step), c), device_id_type=MESH)
 
-    def row_copy(step, owner, h):
-        block = gathered.at[c, owner, h]
+    def row_copy(step, owner, k, p):
+        block = gathered.at[c, owner, k]
         return pltpu.make_async_remote_copy(
             src_ref=block, dst_ref=block,
-            send_sem=row_send.at[step], recv_sem=row_recv.at[step], device_id=across, device_id_type=MESH)
-
-    def core_copy(step, owner, h, side, which):
-        block = gathered.at[side, owner, h]
+            send_sem=row_send.at[p, step], recv_sem=row_recv.at[p, step], device_id=across, device_id_type=MESH)
+
+    def core_copy(step, owner, k, side):
+        block = gathered.at[side, owner, k]
         return pltpu.make_async_remote_copy(
             src_ref=block, dst_ref=block,
-            send_sem=core_send.at[which, step], recv_sem=core_recv.at[which, step],
+            send_sem=core_send.at[k, step], recv_sem=core_recv.at[k, step],
             device_id=sibling, device_id_type=MESH)
 
     def part_copy(step, owner):
@@ -124,17 +131,29 @@
 
     @pl.loop(1, n)
     def _(step):
-        net(step, me).start()
-
-    @pl.loop(1, n)
-    def _(step):
         scale_copy(step, me).start()
 
     mean_copy(c).start()
+
+    @pl.loop(1, quarter)
+    def _(step):
+        for k in range(pieces):
+            net(step, me, k).start()
+
+    @pl.loop(quarter, near)
+    def _(step):
+        for k in mine:
+            net(step, me, k).start()
+
+    @pl.loop(0, near)
+    def _(q):
+        for k in mine:
+            net(far(q), me, k).start()
+
     for copy in own:
         copy.wait()
-    core_copy(0, me, g, c, 0).start()
-    core_copy(0, me, 1 - g, c, 1).start()
+    for k in range(pieces):
+        core_copy(0, me, k, c).start()
 
     seed_terms = seeds[:, pl.ds(pl.multiple_of(c * samples, 128), samples)] * jnp.int32(-1640531527)
     lanes = min(512, samples)
@@ -147,27 +166,25 @@
             counters = ids * jnp.int32(2 * 668265261 - 2**32 if 2 * 668265261 >= 2**31 else 2 * 668265261)
             for start in range(0, samples, lanes):
                 high, low = split(normals(seed_terms[:, start:start + lanes], counters))
-                here = pl.ds(pl.multiple_of(tile * 16, 16), 16)
-                coef_hi[owner, here, start:start + lanes] = high
-                coef_lo[owner, here, start:start + lanes] = low
+                for part, values in enumerate((high, low, high)):
+                    here = pl.ds(pl.multiple_of(part * rows + tile * 16, 16), 16)
+                    coefs[owner, here, start:start + lanes] = values
 
     def multiply(step, owner, first):
-        core_copy(step, owner, g, 1 - c, 0).wait_recv()
-        core_copy(step, owner, 1 - g, 1 - c, 1).wait_recv()
+        for k in range(pieces):
+            core_copy(step, owner, k, 1 - c).wait_recv()
         scale_row = scale_all[owner]
         for side in range(2):
             block = gathered[side, owner].reshape(rows, wide)
             high, low = split(block.T * scale_row)
-            lhs_hi[side * wide:(side + 1) * wide, :] = high
-            lhs_lo[side * wide:(side + 1) * wide, :] = low
-        columns = min(256, samples)
+            for part, values in enumerate((high, high, low)):
+                lhs[side * wide:(side + 1) * wide, part * rows:(part + 1) * rows] = values
+        columns = min(512, samples)
 
         @pl.loop(0, samples // columns)
         def _(tile):
             here = pl.ds(pl.multiple_of(tile * columns, 128), columns)
-            right_hi, right_lo = coef_hi[owner, :, here], coef_lo[owner, :, here]
-            dot = functools.partial(jnp.dot, preferred_element_type=jnp.float32)
-            product = dot(lhs_hi[...], right_hi) + dot(lhs_lo[...], right_hi) + dot(lhs_hi[...], right_lo)
+            product = jnp.dot(lhs[...], coefs[owner, :, here], preferred_element_type=jnp.float32)
             if first:
                 total[:, here] = product
             else:
@@ -175,26 +192,72 @@
 
     draw(me)
 
-    def arrive(step):
-        owner = source(step)
-        net(step, owner).wait_recv()
-        row_copy(step, owner, g).start()
-        core_copy(step, owner, g, c, 0).start()
-        draw(owner)
-        row_copy(step, owner, 1 - g).wait_recv()
-        core_copy(step, owner, 1 - g, c, 1).start()
-
-    arrive(1)
+    def forward(step):
+        owner = to(step)
+        for p, k in enumerate(mine):
+            net(step, owner, k).wait_recv()
+            row_copy(step, owner, k, p).start()
+            core_copy(step, owner, k, c).start()
+
+    def finish(step):
+        owner = to(step)
+        for p, k in enumerate(theirs):
+            row_copy(step, owner, k, p).wait_recv()
+            core_copy(step, owner, k, c).start()
+
+    def use(step):
+        scale_copy(step, to(step)).wait_recv()
+        multiply(step, to(step), False)
+
+    @pl.loop(1, quarter)
+    def _(step):
+        draw(to(step))
+
     multiply(0, me, True)
 
-    @pl.loop(2, n)
-    def _(step):
-        arrive(step)
-        scale_copy(step - 1, source(step - 1)).wait_recv()
-        multiply(step - 1, source(step - 1), False)
-
-    scale_copy(n - 1, source(n - 1)).wait_recv()
-    multiply(n - 1, source(n - 1), False)
+    @pl.loop(0, quarter)
+    def _(q):
+        draw(to(quarter + q))
+        forward(quarter + q)
+        draw(to(far(q)))
+        draw(to(far(quarter + q)))
+        forward(far(q))
+
+    @pl.loop(1, quarter)
+    def _(step):
+        for k in range(pieces):
+            net(step, to(step), k).wait_recv()
+            core_copy(step, to(step), k, c).start()
+
+    @pl.loop(quarter, near)
+    def _(step):
+        finish(step)
+
+    @pl.loop(1, near - quarter // 2)
+    def _(step):
+        use(step)
+
+    @pl.loop(quarter, near)
+    def _(q):
+        forward(far(q))
+
+    @pl.loop(0, quarter)
+    def _(q):
+        finish(far(q))
+
+    @pl.loop(near - quarter // 2, near)
+    def _(step):
+        use(step)
+
+    @pl.loop(0, quarter)
+    def _(q):
+        use(far(q))
+
+    @pl.loop(quarter, near)
+    def _(q):
+        finish(far(q))
+        use(far(q))
+
     mean_copy(1 - c).wait_recv()
 
     sums = jnp.zeros((1, samples), jnp.float32)
@@ -220,7 +283,7 @@
 
     @pl.loop(1, n)
     def _(step):
-        part_copy(step, source(step)).wait_recv()
+        part_copy(step, to(step)).wait_recv()
 
     summed = jnp.zeros((1, samples), jnp.float32)
     for m in range(n):
@@ -232,18 +295,27 @@
     half_copy(c).start()
 
     mean_copy(c).wait_send()
-    core_copy(0, me, g, c, 0).wait_send()
-    core_copy(0, me, 1 - g, c, 1).wait_send()
-
-    @pl.loop(1, n)
-    def _(step):
-        owner = source(step)
-        net(step, me).wait_send()
+    for k in range(pieces):
+        core_copy(0, me, k, c).wait_send()
+
+    @pl.loop(1, n)
+    def _(step):
         scale_copy(step, me).wait_send()
         part_copy(step, me).wait_send()
-        row_copy(step, owner, g).wait_send()
-        core_copy(step, owner, g, c, 0).wait_send()
-        core_copy(step, owner, 1 - g, c, 1).wait_send()
+        for k in range(pieces):
+            core_copy(step, to(step), k, c).wait_send()
+        for k in mine:
+            net(step, me, k).wait_send()
+
+    @pl.loop(1, quarter)
+    def _(step):
+        for k in theirs:
+            net(step, me, k).wait_send()
+
+    @pl.loop(quarter, n)
+    def _(step):
+        for p, k in enumerate(mine):
+            row_copy(step, to(step), k, p).wait_send()
 
     half_copy(1 - c).wait_recv()
     half_copy(c).wait_send()
@@ -257,7 +329,7 @@
 def on_device(mode_basis, mode_scales, mean_log, sample_seeds):
     n = lax.axis_size("mode")
     rows, wide, all_samples = mode_scales.shape[0], mean_log.shape[0], sample_seeds.shape[0]
-    half, samples = rows // 2, all_samples // 2
+    piece, samples = rows // 4, all_samples // 2
     vmem = pl.BlockSpec(memory_space=pltpu.VMEM)
     anywhere = pl.BlockSpec(memory_space=pl.ANY)
     dma = pltpu.SemaphoreType.DMA
@@ -270,19 +342,17 @@
         in_specs=[anywhere, vmem, vmem, vmem],
         out_specs=(anywhere, vmem),
         scratch_shapes=[
-            pltpu.VMEM((2, n, 2, half, wide), jnp.float32),
+            pltpu.VMEM((2, n, 4, piece, wide), jnp.float32),
             pltpu.VMEM((n, 1, rows), jnp.float32),
             pltpu.VMEM((2, 1, wide), jnp.float32),
-            pltpu.VMEM((n, rows, samples), jnp.bfloat16),
-            pltpu.VMEM((n, rows, samples), jnp.bfloat16),
-            pltpu.VMEM((2 * wide, rows), jnp.bfloat16),
-            pltpu.VMEM((2 * wide, rows), jnp.bfloat16),
+            pltpu.VMEM((n, 3 * rows, samples), jnp.bfloat16),
+            pltpu.VMEM((2 * wide, 3 * rows), jnp.bfloat16),
             pltpu.VMEM((2 * wide, samples), jnp.float32),
             pltpu.VMEM((2, wide, samples), jnp.float32),
             pltpu.VMEM((n, 1, samples), jnp.float32),
             pltpu.VMEM((2, 1, samples), jnp.float32),
-            dma((n,)), dma((n,)), dma((n,)), dma((n,)), dma((2, n)), dma((2, n)),
-            dma((n,)), dma((n,)), dma((n,)), dma((n,)), dma((2,)), dma((2,)), dma((3,)), dma((2,)),
+            dma((4, n)), dma((4, n)), dma((2, n)), dma((2, n)), dma((4, n)), dma((4, n)),
+            dma((n,)), dma((n,)), dma((n,)), dma((n,)), dma((2,)), dma((4,)), dma((3,)), dma((2,)),
         ],
         compiler_params=pltpu.CompilerParams(
             collective_id=0, has_side_effects=True, vmem_limit_bytes=60 * 1024 * 1024

time: 111 us -> 79.8 us (0.72)
  Pallas kernels: 107 us -> 75.2 us
    pallas_call x1, Pallas kernels: 107 us -> 75.2 us  [on_device(): pl.pallas_call(functools.partial(kernel, n), out_shape=(jax.ShapeDtypeStr...]
where the time goes in v2:
time: 79.8 us; the launch traced here: 79.6 us
  Pallas kernels  75.2 us (94%)
  local copies, waits for them, and re-layouts  3.74 us (5%)
    pallas_call x1, Pallas kernels, on_device(): pl.pallas_call(functools.partial(kernel, n), out_shape=(jax.ShapeDtypeStr...  75.2 us
    unnamed x4, local copies, waits for them, and re-layouts  3.74 us

profile of v2, /device:TPU:0, one launch (start us, length us, event | category | flops | bytes accessed | tf_op | source)
XLA Modules:
  0.0 79.6 jit_solution(2727282152578280968)
XLA Ops:
  0.6 75.2 %shard_map.59 = (f32[256,2048]{1,0:T(8,128)}, f32[1,2048]{1,0:T(1,128)}) custom-call(f32[512,2048]{1,0:T(8,128)} %basis.1, f32[1,512]{1,0:T(1,128)} %bitcast.6, f32[1,256]{1,0:T(1,128)} %bitcast.7, s32[1,2048]{1,0:T(1,128)} %bitcast.4), custom_call_target="tpu_custom_call" | custom-call | tf_op jit(solution)/shard_map/pallas_call | solution.py:336
  75.8 0.0 copy-start
  75.9 3.1 %copy.8 = f32[256,2048]{1,0:T(8,128)} copy(f32[256,2048]{1,0:T(8,128)} %get-tuple-element.8) | data formatting | bytes 4194304
  79.0 0.0 copy-done
  79.0 0.6 copy.9
Async XLA Ops:
  75.8 3.2 %copy-start = (f32[1,2048]{1,0:T(1,128)S(1)}, f32[1,2048]{1,0:T(1,128)}, u32[]{:S(2)}) copy-start(f32[1,2048]{1,0:T(1,128)} %get-tuple-element.5) | copy-start | bytes 24580

commit v3 on v2

--- a/solution.py
+++ b/solution.py
@@ -179,7 +179,7 @@
             high, low = split(block.T * scale_row)
             for part, values in enumerate((high, high, low)):
                 lhs[side * wide:(side + 1) * wide, part * rows:(part + 1) * rows] = values
-        columns = min(512, samples)
+        columns = min(1024, samples)
 
         @pl.loop(0, samples // columns)
         def _(tile):
@@ -252,10 +252,10 @@
     @pl.loop(0, quarter)
     def _(q):
         use(far(q))
+        finish(far(quarter + q))
 
     @pl.loop(quarter, near)
     def _(q):
-        finish(far(q))
         use(far(q))
 
     mean_copy(1 - c).wait_recv()

time: 79.8 us -> 76.2 us (0.955)
  Pallas kernels: 75.2 us -> 71.6 us
    pallas_call x1, Pallas kernels: 75.2 us -> 71.6 us  [on_device(): pl.pallas_call(functools.partial(kernel, n), out_shape=(jax.ShapeDtypeStr...]
where the time goes in v3:
time: 76.2 us; the launch traced here: 76 us
  Pallas kernels  71.6 us (94%)
  local copies, waits for them, and re-layouts  3.74 us (5%)
    pallas_call x1, Pallas kernels, on_device(): pl.pallas_call(functools.partial(kernel, n), out_shape=(jax.ShapeDtypeStr...  71.6 us
    unnamed x4, local copies, waits for them, and re-layouts  3.74 us

profile of v3, /device:TPU:0, one launch (start us, length us, event | category | flops | bytes accessed | tf_op | source)
XLA Modules:
  0.0 76.0 jit_solution(11960361197375803839)
XLA Ops:
  0.6 71.6 %shard_map.59 = (f32[256,2048]{1,0:T(8,128)}, f32[1,2048]{1,0:T(1,128)}) custom-call(f32[512,2048]{1,0:T(8,128)} %basis.1, f32[1,512]{1,0:T(1,128)} %bitcast.6, f32[1,256]{1,0:T(1,128)} %bitcast.7, s32[1,2048]{1,0:T(1,128)} %bitcast.4), custom_call_target="tpu_custom_call" | custom-call | tf_op jit(solution)/shard_map/pallas_call | solution.py:336
  72.2 0.0 copy-start
  72.2 3.1 %copy.8 = f32[256,2048]{1,0:T(8,128)} copy(f32[256,2048]{1,0:T(8,128)} %get-tuple-element.8) | data formatting | bytes 4194304
  75.4 0.0 copy-done
  75.4 0.6 copy.9
Async XLA Ops:
  72.2 3.2 %copy-start = (f32[1,2048]{1,0:T(1,128)S(1)}, f32[1,2048]{1,0:T(1,128)}, u32[]{:S(2)}) copy-start(f32[1,2048]{1,0:T(1,128)} %get-tuple-element.5) | copy-start | bytes 24580
